TPU v7x, 32 devices: a whole 2x2x4 slice. The times are simulated.
32 devices in a mesh: ep: 4 (over z), tp: 8 (over y, x, core).
Axes of the slice: x: 2, y: 2, z: 4, core: 2. Of those that a mesh axis runs over, the one named last changes fastest.
Arguments:
- tokens: bfloat16 [384, 3072], P('ep', 'tp'), may hold values from -6 to 6
- cotangent: bfloat16 [384, 3072], P('ep', 'tp'), may hold values from -6 to 6
- expert_ids: int32 [384, 2], P('ep'), may hold values from 0 to 3, all different within a row; in each aligned block of 96 rows (0 to 95, 96 to 191, ...) at most 80 rows name the same one
- combine_weights: float32 [384, 2], P('ep'), may hold values from 0.1 to 1
- w_gate: bfloat16 [4, 3072, 8192], P('ep', None, 'tp'), may hold values from -0.15625 to 0.15625
- w_up: bfloat16 [4, 3072, 8192], P('ep', None, 'tp'), may hold values from -0.109375 to 0.109375
- w_down: bfloat16 [4, 8192, 3072], P('ep', 'tp'), may hold values from -0.09375 to 0.09375
Outputs:
- mixed: bfloat16 [384, 3072], P('ep', 'tp')
- grad_tokens: bfloat16 [384, 3072], P('ep', 'tp')
- grad_combine: float32 [384, 2], P('ep')
- grad_gate: bfloat16 [4, 3072, 8192], P('ep', 'tp')
- grad_up: bfloat16 [4, 3072, 8192], P('ep', 'tp')
- grad_down: bfloat16 [4, 8192, 3072], P('ep', None, 'tp')
Inputs may be any that keep to these rules, and one draw needn't show every extreme that they name: `expert_ids`: each row names 2 different experts. Among the 96 rows of one index of ep, no expert is named more than 80 times, and in some such blocks one expert is named exactly 80 times.
All inputs are finite; a program needn't handle non-finite values.
Results may differ from a plain program's by a relative error of at most 0.019.
Values may be sent and summed in bfloat16 or wider, within the bound.
A program may use at most 128 MiB of HBM per device.

v0:
```python
import jax
import jax.numpy as jnp
from jax import lax
from jax.sharding import PartitionSpec as P


def silu_parts(gate_pre):
    sigma = jax.nn.sigmoid(gate_pre)
    return (gate_pre * sigma, sigma * (1.0 + gate_pre * (1.0 - sigma)))


def contract_rows(left, right):
    return lax.dot_general(
        left, right, (((0,), (0,)), ((), ())), preferred_element_type=jnp.float32
    )


def contract_cols(left, right):
    return lax.dot_general(
        left, right, (((1,), (1,)), ((), ())), preferred_element_type=jnp.float32
    )


def body(tokens, cotangent, expert_ids, combine_weights, w_gate, w_up, w_down):
    groups = lax.axis_size("ep")
    tok_rows, piece_width = tokens.shape
    chosen = expert_ids.shape[1]
    capacity = tok_rows * chosen * 5 // (3 * groups)
    buffer_rows = groups * capacity
    gate_weight = w_gate[0]
    up_weight = w_up[0]
    down_weight = w_down[0]
    hidden_width = gate_weight.shape[1]
    flat_ids = expert_ids.reshape(-1)
    onehot = (flat_ids[:, None] == jnp.arange(groups, dtype=jnp.int32)[None, :]).astype(jnp.int32)
    rank = jnp.sum((jnp.cumsum(onehot, axis=0) - onehot) * onehot, axis=1)
    slot_index = flat_ids * capacity + rank
    places = (jnp.arange(buffer_rows, dtype=jnp.int32)[:, None] == slot_index[None, :]).astype(
        jnp.bfloat16
    )
    placer = jnp.sum(
        places.reshape(buffer_rows, tok_rows, chosen).astype(jnp.float32), axis=2
    ).astype(jnp.bfloat16)
    scaled = (combine_weights[:, :, None] * cotangent[:, None, :].astype(jnp.float32)).astype(
        jnp.bfloat16
    )
    send_grad = jnp.dot(
        places, scaled.reshape(tok_rows * chosen, piece_width), preferred_element_type=jnp.float32
    ).astype(jnp.bfloat16)
    send_rows = jnp.dot(placer, tokens, preferred_element_type=jnp.float32).astype(jnp.bfloat16)
    recv_rows, recv_grad = (
        lax.all_to_all(
            send_rows.reshape(groups, capacity, piece_width),
            "ep",
            split_axis=0,
            concat_axis=0,
            tiled=True,
        ),
        lax.all_to_all(
            send_grad.reshape(groups, capacity, piece_width),
            "ep",
            split_axis=0,
            concat_axis=0,
            tiled=True,
        ),
    )
    recv_rows = recv_rows.reshape(buffer_rows, piece_width)
    piece = lax.all_gather(recv_rows, "tp", axis=1, tiled=True)
    gate_pre = jnp.dot(piece, gate_weight, preferred_element_type=jnp.float32)
    up_pre = jnp.dot(piece, up_weight, preferred_element_type=jnp.float32)
    recv_grad = recv_grad.reshape(buffer_rows, piece_width)
    active, slope = silu_parts(gate_pre)
    hidden = (active * up_pre).astype(jnp.bfloat16)
    partial_value = jnp.dot(hidden, down_weight, preferred_element_type=jnp.float32)
    out_piece = lax.psum_scatter(
        partial_value.astype(jnp.bfloat16), "tp", scatter_dimension=1, tiled=True
    )
    out_back = lax.all_to_all(
        out_piece.reshape(groups, capacity, piece_width),
        "ep",
        split_axis=0,
        concat_axis=0,
        tiled=True,
    ).reshape(buffer_rows, piece_width)
    out_tokens = (
        jnp.take(out_back, slot_index, axis=0)
        .reshape(tok_rows, chosen, piece_width)
        .astype(jnp.float32)
    )
    mixed = jnp.sum(combine_weights[:, :, None] * out_tokens, axis=1).astype(jnp.bfloat16)
    local_products = jnp.sum(cotangent.astype(jnp.float32)[:, None, :] * out_tokens, axis=2)
    grad_combine = lax.psum(local_products, "tp")
    grad_hidden = contract_cols(lax.all_gather(recv_grad, "tp", axis=1, tiled=True), down_weight)
    down_grad = contract_rows(hidden, lax.all_gather(recv_grad, "tp", axis=1, tiled=True))
    grad_gate_pre = (grad_hidden * up_pre * slope).astype(jnp.bfloat16)
    grad_up_pre = (grad_hidden * active).astype(jnp.bfloat16)
    input_partial = contract_cols(grad_gate_pre, gate_weight) + contract_cols(
        grad_up_pre, up_weight
    )
    input_piece = lax.psum_scatter(
        input_partial.astype(jnp.bfloat16), "tp", scatter_dimension=1, tiled=True
    )
    input_back = lax.all_to_all(
        input_piece.reshape(groups, capacity, piece_width),
        "ep",
        split_axis=0,
        concat_axis=0,
        tiled=True,
    ).reshape(buffer_rows, piece_width)
    grad_tokens = jnp.sum(
        jnp.take(input_back, slot_index, axis=0)
        .reshape(tok_rows, chosen, piece_width)
        .astype(jnp.float32),
        axis=1,
    ).astype(jnp.bfloat16)
    stacked = jnp.concatenate([grad_gate_pre, grad_up_pre], axis=1)
    both_grads = contract_rows(lax.all_gather(recv_rows, "tp", axis=1, tiled=True), stacked)
    gate_grad = both_grads[:, :hidden_width].astype(jnp.bfloat16)
    up_grad = both_grads[:, hidden_width:].astype(jnp.bfloat16)
    gate_rows_out, up_rows_out = (
        lax.all_to_all(gate_grad, "tp", split_axis=0, concat_axis=1, tiled=True),
        lax.all_to_all(up_grad, "tp", split_axis=0, concat_axis=1, tiled=True),
    )
    down_cols_out = lax.all_to_all(
        down_grad.astype(jnp.bfloat16), "tp", split_axis=1, concat_axis=0, tiled=True
    )
    return (
        mixed,
        grad_tokens,
        grad_combine,
        gate_rows_out[None],
        up_rows_out[None],
        down_cols_out[None],
    )


def solution(mesh):
    placed = (
        P("ep", "tp"),
        P("ep", "tp"),
        P("ep", None),
        P("ep", None),
        P("ep", None, "tp"),
        P("ep", None, "tp"),
        P("ep", "tp", None),
    )
    return jax.shard_map(
        body,
        mesh=mesh,
        in_specs=placed,
        out_specs=(
            P("ep", "tp"),
            P("ep", "tp"),
            P("ep", None),
            P("ep", "tp", None),
            P("ep", "tp", None),
            P("ep", None, "tp"),
        ),
        check_vma=False,
    )
```

profile of v0, /device:TPU:0, one launch (start us, length us, event | category | flops | bytes accessed | tf_op | source)
XLA Modules:
  0.0 508.4 jit_solution(12819426446226769640)
XLA Ops:
  12.3 14.8 %all_to_all.68 = bf16[4,80,384]{2,1,0:T(8,128)(2,1)} all-to-all(bf16[4,80,384]{2,1,0:T(8,128)(2,1)S(1)} %bitcast.77), channel_id=1, replica_groups=mesh['ep'=4,'tp'=8] {'ep'}, dimensions={0} | all-to-all | bytes 491520 | tf_op jit(solution)/shard_map/all_to_all | solution.py:59
  27.8 10.8 %all_to_all.69 = bf16[4,80,384]{2,1,0:T(8,128)(2,1)} all-to-all(bf16[4,80,384]{2,1,0:T(8,128)(2,1)S(1)} %bitcast.78), channel_id=1, replica_groups=mesh['ep'=4,'tp'=8] {'ep'}, dimensions={0} | all-to-all | bytes 491520 | tf_op jit(solution)/shard_map/all_to_all | solution.py:52
  38.6 15.3 %all-gather.5.cloned.1.call-done = bf16[320,3072]{1,0:T(8,128)(2,1)} async-done(((bf16[320,384]{1,0:T(8,128)(2,1)}), bf16[320,3072]{1,0:T(8,128)(2,1)}) %all-gather.5.cloned.1.call-update) | async-done | bytes 1966096 | tf_op jit(solution)/shard_map/all_gather | solution.py:93
  53.9 6.7 %fusion = f32[320,1024]{1,0:T(8,128)} fusion(bf16[320,3072]{1,0:T(8,128)(2,1)} %all-gather.5.cloned.1.call-done, bf16[1,1024,3072]{2,1,0:T(8,128)(2,1)} %param.15), kind=kOutput, calls=%fused_computation.4 | convolution fusion | flops 2013265920 | bytes 9568256 | tf_op jit(solution)/shard_map/dot_general | solution.py:19
  60.6 22.8 %all-gather.3.cloned.1.call-done = bf16[320,3072]{1,0:T(8,128)(2,1)} async-done(((bf16[320,384]{1,0:T(8,128)(2,1)}), bf16[320,3072]{1,0:T(8,128)(2,1)}) %all-gather.3.cloned.1.call-update) | async-done | bytes 1966096 | tf_op jit(solution)/shard_map/all_gather | solution.py:68
  83.3 5.7 %fusion.6 = f32[320,1024]{1,0:T(8,128)S(1)} fusion(bf16[320,3072]{1,0:T(8,128)(2,1)} %all-gather.3.cloned.1.call-done, bf16[1,3072,1024]{2,1,0:T(8,128)(2,1)} %param.14), kind=kOutput, calls=%fused_computation.10 | convolution fusion | flops 2013265920 | bytes 9568256 | tf_op jit(solution)/shard_map/dot_general | solution.py:70
  89.1 5.7 %multiply_convert_fusion.1 = (bf16[320,1024]{1,0:T(8,128)(2,1)S(1)}, bf16[320,1024]{1,0:T(8,128)(2,1)S(1)}, bf16[320,1024]{1,0:T(8,128)(2,1)S(1)}) fusion(f32[320,1024]{1,0:T(8,128)S(1)} %copy-done.6, f32[320,1024]{1,0:T(8,128)S(1)} %fusion.6, bf16[320,3072]{1,0:T(8,128)(2,1)S(1)} %copy-done.4, bf16[1,3072,1024]{2,1,0:T(8,128)(2,1)} %param.13), kind=kOutput, calls=%fused_computation.24 | convolution fusion | flops 2018181120 | bytes 12845056 | tf_op jit(solution)/shard_map/dot_general | solution.py:69
  94.9 2.2 fusion.4
  97.2 2.3 fusion.15
  99.4 2.4 copy.66
  102.1 5.0 fusion.18
  107.1 2.4 copy.64
  109.5 34.8 %reduce-scatter.9.cloned.1.call-done = bf16[384,320]{1,0:T(8,128)(2,1)} async-done(((bf16[3072,320]{1,0:T(8,128)(2,1)}), bf16[384,320]{1,0:T(8,128)(2,1)}) %reduce-scatter.9.cloned.1.call-update) | async-done | bytes 245776
  144.4 1.8 copy.67
  146.2 4.6 all-to-all-start.3
  150.8 10.9 %convolution_convert_fusion = bf16[3072,2048]{1,0:T(8,128)(2,1)} fusion(bf16[320,3072]{1,0:T(8,128)(2,1)S(1)} %copy-done.5, bf16[320,1024]{1,0:T(8,128)(2,1)} %copy-done.8, bf16[320,1024]{1,0:T(8,128)(2,1)} %copy-done.7), kind=kOutput, calls=%fused_computation.2 | convolution fusion | flops 4035444736 | bytes 15859712 | tf_op jit(solution)/shard_map/dot_general | solution.py:13
  161.7 28.8 %reduce-scatter.7.cloned.1.call-done = bf16[384,320]{1,0:T(8,128)(2,1)} async-done(((bf16[3072,320]{1,0:T(8,128)(2,1)}), bf16[384,320]{1,0:T(8,128)(2,1)}) %reduce-scatter.7.cloned.1.call-update) | async-done | bytes 245776
  190.5 1.8 copy.65
  192.3 4.6 all-to-all-start.1
  196.9 10.4 %fusion.32 = (bf16[3072,1024]{1,0:T(8,128)(2,1)}, bf16[3072,1024]{1,0:T(8,128)(2,1)}) fusion(bf16[3072,2048]{1,0:T(8,128)(2,1)} %convolution_convert_fusion), kind=kLoop, calls=%fused_computation.55 | loop fusion | bytes 25165824 | tf_op jit(solution)/shard_map/slice | solution.py:119
  207.4 76.9 %all_to_all.70 = bf16[8,384,1024]{2,1,0:T(8,128)(2,1)} all-to-all(bf16[8,384,1024]{2,1,0:T(8,128)(2,1)} %bitcast.69), channel_id=1, replica_groups=mesh['ep'=4,'tp'=8] {'tp'}, dimensions={0} | all-to-all | bytes 12582912 | tf_op jit(solution)/shard_map/all_to_all | solution.py:121
  284.2 4.9 all-to-all-start.5
  289.1 3.7 convolution_convert_fusion.1
  292.8 3.3 copy.72
  296.1 64.6 %all-to-all-done.5 = bf16[8,384,1024]{2,1,0:T(8,128)(2,1)} async-done(((bf16[8,384,1024]{2,1,0:T(8,128)(2,1)}), bf16[8,384,1024]{2,1,0:T(8,128)(2,1)}, u32[]{:S(2)}, u32[]{:S(2)}) %all-to-all-start.5) | async-done | bytes 6291488 | tf_op jit(solution)/shard_map/all_to_all | solution.py:122
  360.7 4.8 all-to-all-start.6
  368.2 85.9 %psum.7 = f32[96,2]{1,0:T(8,128)S(1)} all-reduce(f32[96,2]{1,0:T(8,128)S(1)} %reduce_sum.61), channel_id=1, replica_groups=mesh['ep'=4,'tp'=8] {'tp'}, use_global_device_ids=true, to_apply=%region_9.11 | all-reduce | flops 192 | bytes 1536 | tf_op jit(solution)/shard_map/psum | solution.py:92
  456.9 9.0 %copy.60 = bf16[384,8,1024]{2,1,0:T(8,128)(2,1)} copy(bf16[384,8,1024]{2,0,1:T(8,128)(2,1)} %bitcast.66) | data formatting | bytes 12582912 | tf_op jit(solution)/shard_map/all_to_all | solution.py:121
  465.9 10.4 %broadcast_in_dim.15 = bf16[1,384,8192]{2,1,0:T(8,128)(2,1)} reshape(bf16[384,8,1024]{2,1,0:T(8,128)(2,1)} %copy.60) | data formatting | bytes 12582912 | tf_op jit(solution)/shard_map/broadcast_in_dim | solution.py:131
  476.3 9.0 %copy.61 = bf16[384,8,1024]{2,1,0:T(8,128)(2,1)} copy(bf16[384,8,1024]{2,0,1:T(8,128)(2,1)} %bitcast.16) | data formatting | bytes 12582912 | tf_op jit(solution)/shard_map/all_to_all | solution.py:122
  485.3 10.4 %broadcast_in_dim.26 = bf16[1,384,8192]{2,1,0:T(8,128)(2,1)} reshape(bf16[384,8,1024]{2,1,0:T(8,128)(2,1)} %copy.61) | data formatting | bytes 12582912 | tf_op jit(solution)/shard_map/broadcast_in_dim | solution.py:132
  495.7 6.1 %copy.75 = bf16[1,8192,384]{2,1,0:T(8,128)(2,1)} copy(bf16[1,8192,384]{2,1,0:T(8,128)(2,1)} %bitcast.18) | data formatting | bytes 12582912
  (76 shorter events, 11.5 us)
Async XLA Ops:
  7.2 20.3 %copy-start = (bf16[96,384]{1,0:T(8,128)(2,1)S(1)}, bf16[96,384]{1,0:T(8,128)(2,1)}, u32[]{:S(2)}) copy-start(bf16[96,384]{1,0:T(8,128)(2,1)} %param.9) | copy-start | bytes 221188
  7.2 20.2 %copy-start.2 = (s32[96,2]{0,1:T(2,128)S(1)}, s32[96,2]{0,1:T(2,128)}, u32[]{:S(2)}) copy-start(s32[96,2]{0,1:T(2,128)} %param.11) | copy-start | bytes 2308
  7.2 46.7 %all-gather.5.cloned.1.call-start = ((), (), s32[]{:S(2)}) async-start(), calls=%async_computation.10 | async-start | bytes 2211840 | tf_op jit(solution)/shard_map/all_gather | solution.py:93
  27.1 56.2 %all-gather.3.cloned.1.call-start = ((), (), s32[]{:S(2)}) async-start(), calls=%async_computation.9 | async-start | bytes 2211840 | tf_op jit(solution)/shard_map/all_gather | solution.py:68
  38.6 105.8 %reduce-scatter.9.cloned.1.call-start = ((), (), s32[]{:S(2)}) async-start(), calls=%async_computation.12 | async-start | bytes 2654208
  83.3 5.7 %copy-start.4 = (bf16[320,3072]{1,0:T(8,128)(2,1)S(1)}, bf16[320,3072]{1,0:T(8,128)(2,1)}, u32[]{:S(2)}) copy-start(bf16[320,3072]{1,0:T(8,128)(2,1)} %all-gather.3.cloned.1.call-done) | copy-start | bytes 5898244
  83.3 5.7 %copy-start.6 = (f32[320,1024]{1,0:T(8,128)S(1)}, f32[320,1024]{1,0:T(8,128)}, u32[]{:S(2)}) copy-start(f32[320,1024]{1,0:T(8,128)} %fusion) | copy-start | bytes 3932164
  83.3 11.5 %slice-start = ((s8[6291456]{0:T(1024)(128)(4,1)}), s8[4194304]{0:T(1024)(128)(4,1)S(1)}, s32[]{:S(2)}) async-start(s8[6291456]{0:T(1024)(128)(4,1)} %bitcast.83), calls=%async_computation.13 | async-start | bytes 8388608
  83.3 13.8 %slice-start.2 = ((s8[6291456]{0:T(1024)(128)(4,1)}), s8[4194304]{0:T(1024)(128)(4,1)S(1)}, s32[]{:S(2)}) async-start(s8[6291456]{0:T(1024)(128)(4,1)} %bitcast.85), calls=%async_computation.15 | async-start | bytes 8388608
  89.1 5.8 %slice-start.1 = ((s8[6291456]{0:T(1024)(128)(4,1)}), s8[2097152]{0:T(1024)(128)(4,1)S(1)}, s32[]{:S(2)}) async-start(s8[6291456]{0:T(1024)(128)(4,1)} %bitcast.83), calls=%async_computation.14 | async-start | bytes 4194304
  89.1 8.1 %slice-start.3 = ((s8[6291456]{0:T(1024)(128)(4,1)}), s8[2097152]{0:T(1024)(128)(4,1)S(1)}, s32[]{:S(2)}) async-start(s8[6291456]{0:T(1024)(128)(4,1)} %bitcast.85), calls=%async_computation.16 | async-start | bytes 4194304
  94.8 2.3 copy-start.8
  94.8 2.3 copy-start.7
  101.9 88.6 %reduce-scatter.7.cloned.1.call-start = ((), (), s32[]{:S(2)}) async-start(), calls=%async_computation.11 | async-start | bytes 2654208
  109.5 41.3 %copy-start.5 = (bf16[320,3072]{1,0:T(8,128)(2,1)S(1)}, bf16[320,3072]{1,0:T(8,128)(2,1)}, u32[]{:S(2)}) copy-start(bf16[320,3072]{1,0:T(8,128)(2,1)} %all-gather.3.cloned.1.call-done) | copy-start | bytes 5898244
  146.2 46.2 %all-to-all-start.3 = ((bf16[4,80,384]{2,1,0:T(8,128)(2,1)}), bf16[4,80,384]{2,1,0:T(8,128)(2,1)S(1)}, u32[]{:S(2)}, u32[]{:S(2)}) async-start(bf16[4,80,384]{2,1,0:T(8,128)(2,1)} %bitcast.11), calls=%async_computation.3 | async-start | bytes 491520 | tf_op jit(solution)/shard_map/all_to_all | solution.py:103
  192.3 15.0 %all-to-all-start.1 = ((bf16[4,80,384]{2,1,0:T(8,128)(2,1)}), bf16[4,80,384]{2,1,0:T(8,128)(2,1)S(1)}, u32[]{:S(2)}, u32[]{:S(2)}) async-start(bf16[4,80,384]{2,1,0:T(8,128)(2,1)} %bitcast.7), calls=%async_computation.1 | async-start | bytes 491520 | tf_op jit(solution)/shard_map/all_to_all | solution.py:78
  284.2 4.9 copy-start.3
  284.2 76.5 %all-to-all-start.5 = ((bf16[8,384,1024]{2,1,0:T(8,128)(2,1)}), bf16[8,384,1024]{2,1,0:T(8,128)(2,1)}, u32[]{:S(2)}, u32[]{:S(2)}) async-start(bf16[8,384,1024]{2,1,0:T(8,128)(2,1)} %bitcast.68), calls=%async_computation.5 | async-start | bytes 12582912 | tf_op jit(solution)/shard_map/all_to_all | solution.py:122
  360.7 135.0 %all-to-all-start.6 = ((bf16[1024,8,384]{2,0,1:T(8,128)(2,1)}), bf16[1024,8,384]{2,0,1:T(8,128)(2,1)}, u32[]{:S(2)}, u32[]{:S(2)}) async-start(bf16[1024,8,384]{2,0,1:T(8,128)(2,1)} %bitcast.67), calls=%async_computation.6 | async-start | bytes 12582912 | tf_op jit(solution)/shard_map/all_to_all | solution.py:124
  495.7 6.2 %copy-start.1 = (bf16[96,384]{1,0:T(8,128)(2,1)S(1)}, bf16[96,384]{1,0:T(8,128)(2,1)}, u32[]{:S(2)}) copy-start(bf16[96,384]{1,0:T(8,128)(2,1)} %param.9) | copy-start | bytes 221188
Sparse Core Ops, SparseCore 0:
  27.2 26.6 all-gather.4
  55.8 27.5 all-gather.2
  102.0 42.3 reduce-scatter.8
  148.2 42.3 reduce-scatter.6
where the time goes:
time: 510 us; the launch traced here: 508 us
  blocking collectives  188 us (37%)
  waiting for transfers between devices  166 us (33%)
  local copies, waits for them, and re-layouts  73.7 us (14%)
  matrix products  42.8 us (8%)
  starting transfers between devices  19.2 us (4%)
  between operations  14.1 us (3%)
    psum x1, blocking collectives, body(): grad_combine = lax.psum(local_products, 'tp')  85.9 us
    all_to_all x1, blocking collectives, body(): lax.all_to_all(gate_grad, 'tp', split_axis=0, concat_axis=1, tiled=True)  76.9 us
    all_to_all x1, waiting for transfers between devices, body(): lax.all_to_all(up_grad, 'tp', split_axis=0, concat_axis=1, tiled=True)  64.6 us
    unnamed x6, waiting for transfers between devices  63.7 us
    all_gather x1, waiting for transfers between devices, body(): piece = lax.all_gather(recv_rows, 'tp', axis=1, tiled=True)  22.8 us
    unnamed x35, local copies, waits for them, and re-layouts  16.9 us
    all_gather x1, waiting for transfers between devices, body(): lax.all_gather(recv_grad, 'tp', axis=1, tiled=True)  15.3 us
    all_to_all x1, blocking collectives, body(): lax.all_to_all(send_grad.reshape(groups, capacity, piece_width), 'ep', sp...  14.8 us
  transfers between devices with their start and end apart: 8, of which 5 were waited for; matrix products, arithmetic and copies ran while one was open for 18% of the time, Pallas kernels for 0%

commit v1 on v0

--- a/solution.py
+++ b/solution.py
@@ -30,7 +30,6 @@
     gate_weight = w_gate[0]
     up_weight = w_up[0]
     down_weight = w_down[0]
-    hidden_width = gate_weight.shape[1]
     flat_ids = expert_ids.reshape(-1)
     onehot = (flat_ids[:, None] == jnp.arange(groups, dtype=jnp.int32)[None, :]).astype(jnp.int32)
     rank = jnp.sum((jnp.cumsum(onehot, axis=0) - onehot) * onehot, axis=1)
@@ -91,7 +90,6 @@
     local_products = jnp.sum(cotangent.astype(jnp.float32)[:, None, :] * out_tokens, axis=2)
     grad_combine = lax.psum(local_products, "tp")
     grad_hidden = contract_cols(lax.all_gather(recv_grad, "tp", axis=1, tiled=True), down_weight)
-    down_grad = contract_rows(hidden, lax.all_gather(recv_grad, "tp", axis=1, tiled=True))
     grad_gate_pre = (grad_hidden * up_pre * slope).astype(jnp.bfloat16)
     grad_up_pre = (grad_hidden * active).astype(jnp.bfloat16)
     input_partial = contract_cols(grad_gate_pre, gate_weight) + contract_cols(
@@ -113,17 +111,15 @@
         .astype(jnp.float32),
         axis=1,
     ).astype(jnp.bfloat16)
-    stacked = jnp.concatenate([grad_gate_pre, grad_up_pre], axis=1)
-    both_grads = contract_rows(lax.all_gather(recv_rows, "tp", axis=1, tiled=True), stacked)
-    gate_grad = both_grads[:, :hidden_width].astype(jnp.bfloat16)
-    up_grad = both_grads[:, hidden_width:].astype(jnp.bfloat16)
-    gate_rows_out, up_rows_out = (
-        lax.all_to_all(gate_grad, "tp", split_axis=0, concat_axis=1, tiled=True),
-        lax.all_to_all(up_grad, "tp", split_axis=0, concat_axis=1, tiled=True),
-    )
-    down_cols_out = lax.all_to_all(
-        down_grad.astype(jnp.bfloat16), "tp", split_axis=1, concat_axis=0, tiled=True
-    )
+    down_cols_out = contract_rows(
+        lax.all_gather(hidden, "tp", axis=1, tiled=True), recv_grad
+    ).astype(jnp.bfloat16)
+    gate_rows_out = contract_rows(
+        recv_rows, lax.all_gather(grad_gate_pre, "tp", axis=1, tiled=True)
+    ).astype(jnp.bfloat16)
+    up_rows_out = contract_rows(
+        recv_rows, lax.all_gather(grad_up_pre, "tp", axis=1, tiled=True)
+    ).astype(jnp.bfloat16)
     return (
         mixed,
         grad_tokens,

time: 510 us -> 346 us (0.68)
  blocking collectives: 188 us -> 49.5 us
  local copies, waits for them, and re-layouts: 73.7 us -> 15 us
  waiting for transfers between devices: 166 us -> 189 us
  matrix products: 42.8 us -> 63.6 us
  starting transfers between devices: 19.2 us -> 9.68 us
    all_to_all x1 -> x0, blocking collectives: 76.9 us -> none  [body(): lax.all_to_all(gate_grad, 'tp', split_axis=0, concat_axis=1, tiled=True)]
    all_gather x0 -> x3, waiting for transfers between devices: none -> 68.4 us  [the longest x1 34 us: body(): lax.all_gather(hidden, 'tp', axis=1, tiled=True)]
    all_to_all x2 -> x0, waiting for transfers between devices: 64.6 us -> none  [the longest x1 64.6 us: body(): lax.all_to_all(up_grad, 'tp', split_axis=0, concat_axis=1, tiled=True)]
    psum x1, blocking collectives: 85.9 us -> 24 us  [body(): grad_combine = lax.psum(local_products, 'tp')]
    all_to_all x3 -> x0, local copies, waits for them, and re-layouts: 21.3 us -> none  [the longest x1 9 us: body(): lax.all_to_all(gate_grad, 'tp', split_axis=0, concat_axis=1, tiled=True)]
    broadcast_in_dim x2 -> x0, local copies, waits for them, and re-layouts: 20.8 us -> none  [the longest x1 10.4 us: body(): up_rows_out[None]]
    dot_general x2 -> x3, matrix products: 14.6 us -> 26.6 us  [contract_rows(): lax.dot_general(left, right, (((0,), (0,)), ((), ())), preferred_element_...]
    unnamed x6 -> x9, waiting for transfers between devices: 63.7 us -> 74.4 us
  transfers between devices with their start and end apart: 8 -> 9, of which waited for: 5 -> 8; matrix products, arithmetic and copies ran while one was open for 18% -> 12% of each run, Pallas kernels for 0% -> 0%
where the time goes in v1:
time: 346 us; the launch traced here: 345 us
  waiting for transfers between devices  189 us (55%)
  matrix products  63.6 us (18%)
  blocking collectives  49.5 us (14%)
  local copies, waits for them, and re-layouts  15 us (4%)
  between operations  14.3 us (4%)
  starting transfers between devices  9.68 us (3%)
  other arithmetic  4.55 us (1%)
    unnamed x9, waiting for transfers between devices  74.4 us
    all_gather x1, waiting for transfers between devices, body(): lax.all_gather(hidden, 'tp', axis=1, tiled=True)  34 us
    all_gather x1, waiting for transfers between devices, body(): lax.all_gather(grad_up_pre, 'tp', axis=1, tiled=True)  33.6 us
    dot_general x3, matrix products, contract_rows(): lax.dot_general(left, right, (((0,), (0,)), ((), ())), preferred_element_...  26.6 us
    psum x1, blocking collectives, body(): grad_combine = lax.psum(local_products, 'tp')  24 us
    all_gather x1, waiting for transfers between devices, body(): piece = lax.all_gather(recv_rows, 'tp', axis=1, tiled=True)  23.8 us
    dot_general x3, matrix products, contract_cols(): lax.dot_general(left, right, (((1,), (1,)), ((), ())), preferred_element_...  19.1 us
    all_to_all x1, blocking collectives, body(): lax.all_to_all(send_grad.reshape(groups, capacity, piece_width), 'ep', sp...  14.8 us
  transfers between devices with their start and end apart: 9, of which 8 were waited for; matrix products, arithmetic and copies ran while one was open for 12% of the time, Pallas kernels for 0%

profile of v1, /device:TPU:0, one launch (start us, length us, event | category | flops | bytes accessed | tf_op | source)
XLA Modules:
  0.0 345.3 jit_solution(14254782053761471952)
XLA Ops:
  7.2 0.8 copy.43
  8.2 1.2 reduce-window.6
  9.9 1.0 mul.83
  12.3 14.8 %all_to_all.20 = bf16[4,80,384]{2,1,0:T(8,128)(2,1)} all-to-all(bf16[4,80,384]{2,1,0:T(8,128)(2,1)S(1)} %bitcast.73), channel_id=1, replica_groups=mesh['ep'=4,'tp'=8] {'ep'}, dimensions={0} | all-to-all | bytes 491520 | tf_op jit(solution)/shard_map/all_to_all | solution.py:58
  28.4 10.8 %all_to_all.21 = bf16[4,80,384]{2,1,0:T(8,128)(2,1)} all-to-all(bf16[4,80,384]{2,1,0:T(8,128)(2,1)S(1)} %bitcast.74), channel_id=1, replica_groups=mesh['ep'=4,'tp'=8] {'ep'}, dimensions={0} | all-to-all | bytes 491520 | tf_op jit(solution)/shard_map/all_to_all | solution.py:51
  39.3 14.6 %all-gather.8.cloned.1.call-done = bf16[320,3072]{1,0:T(8,128)(2,1)} async-done(((bf16[320,384]{1,0:T(8,128)(2,1)}), bf16[320,3072]{1,0:T(8,128)(2,1)}) %all-gather.8.cloned.1.call-update) | async-done | bytes 1966096 | tf_op jit(solution)/shard_map/all_gather | solution.py:92
  53.9 5.6 %fusion.3 = f32[320,1024]{1,0:T(8,128)S(1)} fusion(bf16[320,3072]{1,0:T(8,128)(2,1)} %all-gather.8.cloned.1.call-done, bf16[1,1024,3072]{2,1,0:T(8,128)(2,1)} %param.15), kind=kOutput, calls=%fused_computation.8 | convolution fusion | flops 2013265920 | bytes 9568256 | tf_op jit(solution)/shard_map/dot_general | solution.py:19
  59.5 23.8 %all-gather.6.cloned.1.call-done = bf16[320,3072]{1,0:T(8,128)(2,1)} async-done(((bf16[320,384]{1,0:T(8,128)(2,1)}), bf16[320,3072]{1,0:T(8,128)(2,1)}) %all-gather.6.cloned.1.call-update) | async-done | bytes 1966096 | tf_op jit(solution)/shard_map/all_gather | solution.py:67
  83.3 5.7 %fusion.9 = f32[320,1024]{1,0:T(8,128)S(1)} fusion(bf16[320,3072]{1,0:T(8,128)(2,1)} %all-gather.6.cloned.1.call-done, bf16[1,3072,1024]{2,1,0:T(8,128)(2,1)} %param.14), kind=kOutput, calls=%fused_computation.14 | convolution fusion | flops 2013265920 | bytes 9568256 | tf_op jit(solution)/shard_map/dot_general | solution.py:69
  89.0 6.6 %multiply_convert_fusion.1 = (bf16[320,1024]{1,0:T(8,128)(2,1)}, bf16[320,1024]{1,0:T(8,128)(2,1)S(1)}, bf16[320,1024]{1,0:T(8,128)(2,1)}) fusion(f32[320,1024]{1,0:T(8,128)S(1)} %fusion.3, f32[320,1024]{1,0:T(8,128)S(1)} %fusion.9, bf16[320,3072]{1,0:T(8,128)(2,1)S(1)} %copy-done.6, bf16[1,3072,1024]{2,1,0:T(8,128)(2,1)} %param.13), kind=kOutput, calls=%fused_computation.24 | convolution fusion | flops 2018181120 | bytes 12845056 | tf_op jit(solution)/shard_map/dot_general | solution.py:68
  95.6 7.2 %fusion.7 = f32[320,3072]{1,0:T(8,128)} fusion(bf16[320,1024]{1,0:T(8,128)(2,1)S(1)} %get-tuple-element.34, bf16[1,3072,1024]{2,1,0:T(8,128)(2,1)} %param.14), kind=kOutput, calls=%fused_computation.12 | convolution fusion | flops 2013265920 | bytes 10878976 | tf_op jit(solution)/shard_map/dot_general | solution.py:19
  102.8 6.3 %fusion.18 = bf16[320,3072]{1,0:T(8,128)(2,1)S(1)} fusion(f32[320,3072]{1,0:T(8,128)} %fusion.7, bf16[320,1024]{1,0:T(8,128)(2,1)} %get-tuple-element.33, bf16[1,3072,1024]{2,1,0:T(8,128)(2,1)} %param.13), kind=kOutput, calls=%fused_computation.21 | convolution fusion | flops 2015232000 | bytes 12845056 | tf_op jit(solution)/shard_map/dot_general | solution.py:19
  109.1 2.4 copy.51
  111.8 5.0 %fusion.21 = bf16[320,3072]{1,0:T(8,128)(2,1)S(1)} fusion(bf16[320,1024]{1,0:T(8,128)(2,1)S(1)} %copy-done.5, bf16[1,1024,3072]{2,1,0:T(8,128)(2,1)} %param.15), kind=kOutput, calls=%fused_computation.22 | convolution fusion | flops 2014248960 | bytes 8912896 | tf_op jit(solution)/shard_map/dot_general | solution.py:73
  116.8 2.4 copy.49
  121.2 32.9 %reduce-scatter.9.cloned.1.call-done = bf16[384,320]{1,0:T(8,128)(2,1)} async-done(((bf16[3072,320]{1,0:T(8,128)(2,1)}), bf16[384,320]{1,0:T(8,128)(2,1)}) %reduce-scatter.9.cloned.1.call-update) | async-done | bytes 245776
  154.1 1.8 copy.52
  155.9 4.6 %all-to-all-start.3 = ((bf16[4,80,384]{2,1,0:T(8,128)(2,1)}), bf16[4,80,384]{2,1,0:T(8,128)(2,1)S(1)}, u32[]{:S(2)}, u32[]{:S(2)}) async-start(bf16[4,80,384]{2,1,0:T(8,128)(2,1)} %bitcast.11), calls=%async_computation.3 | async-start | bytes 491520 | tf_op jit(solution)/shard_map/all_to_all | solution.py:101
  160.5 39.7 %reduce-scatter.7.cloned.1.call-done = bf16[384,320]{1,0:T(8,128)(2,1)} async-done(((bf16[3072,320]{1,0:T(8,128)(2,1)}), bf16[384,320]{1,0:T(8,128)(2,1)}) %reduce-scatter.7.cloned.1.call-update) | async-done | bytes 245776
  200.2 1.8 copy.50
  202.0 4.6 %all-to-all-start.1 = ((bf16[4,80,384]{2,1,0:T(8,128)(2,1)}), bf16[4,80,384]{2,1,0:T(8,128)(2,1)S(1)}, u32[]{:S(2)}, u32[]{:S(2)}) async-start(bf16[4,80,384]{2,1,0:T(8,128)(2,1)} %bitcast.7), calls=%async_computation.1 | async-start | bytes 491520 | tf_op jit(solution)/shard_map/all_to_all | solution.py:77
  206.7 1.0 gather_fusion.1
  207.7 7.3 %all-to-all-done.1 = bf16[4,80,384]{2,1,0:T(8,128)(2,1)S(1)} async-done(((bf16[4,80,384]{2,1,0:T(8,128)(2,1)}), bf16[4,80,384]{2,1,0:T(8,128)(2,1)S(1)}, u32[]{:S(2)}, u32[]{:S(2)}) %all-to-all-start.1) | async-done | bytes 245792 | tf_op jit(solution)/shard_map/all_to_all | solution.py:77
  215.0 1.0 gather_fusion
  216.7 24.0 %psum.7 = f32[96,2]{1,0:T(8,128)S(1)} all-reduce(f32[96,2]{1,0:T(8,128)S(1)} %reduce_sum.61), channel_id=1, replica_groups=mesh['ep'=4,'tp'=8] {'tp'}, use_global_device_ids=true, to_apply=%region_9.11 | all-reduce | flops 192 | bytes 1536 | tf_op jit(solution)/shard_map/psum | solution.py:91
  241.3 1.0 reduce_sum.59
  242.3 1.1 multiply_reduce_fusion.1
  244.2 8.7 %fusion = bf16[1,384,8192]{2,1,0:T(8,128)(2,1)} fusion(bf16[320,384]{1,0:T(8,128)(2,1)S(1)} %bitcast.69, bf16[320,8192]{1,0:T(8,128)(2,1)} %all-gather.10.cloned.1.call-done), kind=kOutput, calls=%fused_computation.5 | convolution fusion | flops 2016411648 | bytes 11780096 | tf_op jit(solution)/shard_map/dot_general | solution.py:13
  252.8 34.0 %all-gather.14.cloned.1.call-done = bf16[320,8192]{1,0:T(8,128)(2,1)} async-done(((bf16[320,1024]{1,0:T(8,128)(2,1)}), bf16[320,8192]{1,0:T(8,128)(2,1)}) %all-gather.14.cloned.1.call-update) | async-done | bytes 5242896 | tf_op jit(solution)/shard_map/all_gather | solution.py:115
  286.8 9.3 %fusion.2 = bf16[1,8192,384]{2,1,0:T(8,128)(2,1)} fusion(bf16[320,8192]{1,0:T(8,128)(2,1)} %all-gather.14.cloned.1.call-done, bf16[320,384]{1,0:T(8,128)(2,1)S(1)} %bitcast.72), kind=kOutput, calls=%fused_computation.7 | convolution fusion | flops 2016411648 | bytes 11780096 | tf_op jit(solution)/shard_map/dot_general | solution.py:13
  296.2 33.6 %all-gather.12.cloned.1.call-done = bf16[320,8192]{1,0:T(8,128)(2,1)} async-done(((bf16[320,1024]{1,0:T(8,128)(2,1)}), bf16[320,8192]{1,0:T(8,128)(2,1)}) %all-gather.12.cloned.1.call-update) | async-done | bytes 5242896 | tf_op jit(solution)/shard_map/all_gather | solution.py:121
  329.8 8.7 %fusion.1 = bf16[1,384,8192]{2,1,0:T(8,128)(2,1)} fusion(bf16[320,384]{1,0:T(8,128)(2,1)S(1)} %bitcast.70, bf16[320,8192]{1,0:T(8,128)(2,1)} %all-gather.12.cloned.1.call-done), kind=kOutput, calls=%fused_computation.6 | convolution fusion | flops 2016411648 | bytes 11780096 | tf_op jit(solution)/shard_map/dot_general | solution.py:13
  (60 shorter events, 7.7 us)
Async XLA Ops:
  7.2 21.0 %copy-start = (bf16[96,384]{1,0:T(8,128)(2,1)S(1)}, bf16[96,384]{1,0:T(8,128)(2,1)}, u32[]{:S(2)}) copy-start(bf16[96,384]{1,0:T(8,128)(2,1)} %param.9) | copy-start | bytes 221188
  7.2 46.7 %all-gather.8.cloned.1.call-start = ((), (), s32[]{:S(2)}) async-start(), calls=%async_computation.7 | async-start | bytes 2211840 | tf_op jit(solution)/shard_map/all_gather | solution.py:92
  27.1 56.2 %all-gather.6.cloned.1.call-start = ((), (), s32[]{:S(2)}) async-start(), calls=%async_computation.6 | async-start | bytes 2211840 | tf_op jit(solution)/shard_map/all_gather | solution.py:67
  39.2 114.9 %reduce-scatter.9.cloned.1.call-start = ((), (), s32[]{:S(2)}) async-start(), calls=%async_computation.12 | async-start | bytes 2654208
  83.3 5.7 %copy-start.6 = (bf16[320,3072]{1,0:T(8,128)(2,1)S(1)}, bf16[320,3072]{1,0:T(8,128)(2,1)}, u32[]{:S(2)}) copy-start(bf16[320,3072]{1,0:T(8,128)(2,1)} %all-gather.6.cloned.1.call-done) | copy-start | bytes 5898244
  95.6 7.2 %copy-start.4 = (bf16[320,1024]{1,0:T(8,128)(2,1)}, bf16[320,1024]{1,0:T(8,128)(2,1)S(1)}, u32[]{:S(2)}) copy-start(bf16[320,1024]{1,0:T(8,128)(2,1)S(1)} %get-tuple-element.34) | copy-start | bytes 1966084
  109.1 2.7 copy-start.5
  111.6 88.6 %reduce-scatter.7.cloned.1.call-start = ((), (), s32[]{:S(2)}) async-start(), calls=%async_computation.11 | async-start | bytes 2654208
  119.2 124.9 %all-gather.10.cloned.1.call-start = ((), (), s32[]{:S(2)}) async-start(), calls=%async_computation.8 | async-start | bytes 5898240 | tf_op jit(solution)/shard_map/all_gather | solution.py:118
  119.8 167.0 %all-gather.14.cloned.1.call-start = ((), (), s32[]{:S(2)}) async-start(), calls=%async_computation.10 | async-start | bytes 5898240 | tf_op jit(solution)/shard_map/all_gather | solution.py:115
  120.4 209.3 %all-gather.12.cloned.1.call-start = ((), (), s32[]{:S(2)}) async-start(), calls=%async_computation.9 | async-start | bytes 5898240 | tf_op jit(solution)/shard_map/all_gather | solution.py:121
  121.2 123.0 %copy-start.2 = (bf16[4,80,384]{2,1,0:T(8,128)(2,1)S(1)}, bf16[4,80,384]{2,1,0:T(8,128)(2,1)}, u32[]{:S(2)}) copy-start(bf16[4,80,384]{2,1,0:T(8,128)(2,1)} %all_to_all.21) | copy-start | bytes 737284
  155.9 46.2 %all-to-all-start.3 = ((bf16[4,80,384]{2,1,0:T(8,128)(2,1)}), bf16[4,80,384]{2,1,0:T(8,128)(2,1)S(1)}, u32[]{:S(2)}, u32[]{:S(2)}) async-start(bf16[4,80,384]{2,1,0:T(8,128)(2,1)} %bitcast.11), calls=%async_computation.3 | async-start | bytes 491520 | tf_op jit(solution)/shard_map/all_to_all | solution.py:101
  202.0 13.0 %all-to-all-start.1 = ((bf16[4,80,384]{2,1,0:T(8,128)(2,1)}), bf16[4,80,384]{2,1,0:T(8,128)(2,1)S(1)}, u32[]{:S(2)}, u32[]{:S(2)}) async-start(bf16[4,80,384]{2,1,0:T(8,128)(2,1)} %bitcast.7), calls=%async_computation.1 | async-start | bytes 491520 | tf_op jit(solution)/shard_map/all_to_all | solution.py:77
  243.4 43.5 %copy-start.3 = (bf16[4,80,384]{2,1,0:T(8,128)(2,1)S(1)}, bf16[4,80,384]{2,1,0:T(8,128)(2,1)}, u32[]{:S(2)}) copy-start(bf16[4,80,384]{2,1,0:T(8,128)(2,1)} %all_to_all.20) | copy-start | bytes 737284
  286.8 51.6 %copy-start.1 = (bf16[96,384]{1,0:T(8,128)(2,1)S(1)}, bf16[96,384]{1,0:T(8,128)(2,1)}, u32[]{:S(2)}) copy-start(bf16[96,384]{1,0:T(8,128)(2,1)} %param.9) | copy-start | bytes 221188
Sparse Core Ops, SparseCore 0:
  27.2 26.6 all-gather.7
  55.7 27.5 all-gather.5
  111.7 42.3 reduce-scatter.8
  157.8 42.3 reduce-scatter.6
  202.5 41.5 all-gather.9
  245.9 40.8 all-gather.13
  288.7 40.9 all-gather.11

commit v2 on v1

--- a/solution.py
+++ b/solution.py
@@ -1,7 +1,246 @@
+import functools
+import math
+
 import jax
 import jax.numpy as jnp
 from jax import lax
+from jax.experimental import pallas as pl
+from jax.experimental.pallas import tpu as pltpu
 from jax.sharding import PartitionSpec as P
+
+MESH = pl.DeviceIdType.MESH
+BF = jnp.bfloat16
+
+
+def ring_order(chips):
+    side_x = math.isqrt(chips)
+    side_x = side_x if side_x * side_x == chips else chips // 2
+    side_y = chips // side_x
+    order = [x for x in range(side_x)]
+    for y in range(1, side_y):
+        xs = range(side_x - 1, 0, -1) if y % 2 else range(1, side_x)
+        order += [y * side_x + x for x in xs]
+    order += [y * side_x for y in range(side_y - 1, 0, -1)]
+    return order
+
+
+def pick(table, index):
+    value = jnp.int32(table[0])
+    for i in range(1, len(table)):
+        value = jnp.where(index == i, jnp.int32(table[i]), value)
+    return value
+
+
+def remote(src, dst, send, recv, device):
+    return pltpu.make_async_remote_copy(
+        src_ref=src,
+        dst_ref=dst,
+        send_sem=send,
+        recv_sem=recv,
+        device_id={"tp": device},
+        device_id_type=MESH,
+    )
+
+
+def greet(devices):
+    barrier = pltpu.get_barrier_semaphore()
+    for device in devices:
+        pl.semaphore_signal(barrier, inc=1, device_id={"tp": device}, device_id_type=MESH)
+    pl.semaphore_wait(barrier, len(devices))
+
+
+def gather_kernel(count, chips, *refs):
+    own, out = refs[:count], refs[count : 2 * count]
+    ring_send, ring_recv, core_send, core_recv, keep = refs[2 * count :]
+    order = ring_order(chips)
+    place = [order.index(chip) for chip in range(chips)]
+    me = lax.axis_index("tp")
+    chip, core = me // 2, me % 2
+    spot = pick(place, chip)
+    partner = chip * 2 + 1 - core
+    steps = chips // 2
+    rows = own[0].shape[0]
+    half = rows // 2
+
+    def at(offset):
+        return pick(order, (spot + offset + chips) % chips) * 2 + core
+
+    right, left = at(1), at(-1)
+    greet([right, left, partner])
+
+    def part(ref, way, step):
+        if step < steps - 1:
+            return ref
+        return ref.at[pl.ds(way * half, half)]
+
+    def hop(k, way, step):
+        index = at(-step if way == 0 else step)
+        source = own[k] if step == 0 else out[k].at[index]
+        return remote(
+            part(source, way, step),
+            part(out[k].at[index], way, step),
+            ring_send.at[k, way, step],
+            ring_recv.at[k, way, step],
+            right if way == 0 else left,
+        )
+
+    def arrived(k, way, step):
+        index = at(-(step + 1) if way == 0 else step + 1)
+        block = part(out[k].at[index], way, step)
+        return remote(
+            block, block, ring_send.at[k, way, step], ring_recv.at[k, way, step], right if way == 0 else left
+        ), remote(
+            block, block, core_send.at[k, way, step], core_recv.at[k, way, step], partner
+        )
+
+    def own_pass(k):
+        return remote(
+            own[k], out[k].at[me], core_send.at[k, 2, 0], core_recv.at[k, 2, 0], partner
+        )
+
+    def own_keep(k):
+        return pltpu.make_async_copy(own[k], out[k].at[me], keep.at[k])
+
+    for k in range(count):
+        for way in range(2):
+            hop(k, way, 0).start()
+    for k in range(count):
+        own_pass(k).start()
+        own_keep(k).start()
+    for step in range(steps):
+        for k in range(count):
+            for way in range(2):
+                landed, handed = arrived(k, way, step)
+                landed.wait_recv()
+                if step + 1 < steps:
+                    hop(k, way, step + 1).start()
+                handed.start()
+    for k in range(count):
+        own_keep(k).wait()
+        own_pass(k).wait_send()
+        other = remote(
+            own[k], out[k].at[partner], core_send.at[k, 2, 0], core_recv.at[k, 2, 0], partner
+        )
+        other.wait_recv()
+        for way in range(2):
+            for step in range(steps):
+                hop(k, way, step).wait_send()
+                handed = arrived(k, way, step)[1]
+                handed.wait_send()
+                index = at(-(step + 1) if way == 0 else step + 1) // 2 * 2 + 1 - core
+                block = part(out[k].at[index], way, step)
+                remote(
+                    block, block, core_send.at[k, way, step], core_recv.at[k, way, step], partner
+                ).wait_recv()
+
+
+def gather(arrays, ident):
+    size = lax.axis_size("tp")
+    chips, count = size // 2, len(arrays)
+    ring = pltpu.SemaphoreType.DMA((count, 2, chips // 2))
+    cores = pltpu.SemaphoreType.DMA((count, 3, chips // 2))
+    return pl.pallas_call(
+        functools.partial(gather_kernel, count, chips),
+        out_shape=[jax.ShapeDtypeStruct((size,) + a.shape, a.dtype) for a in arrays],
+        in_specs=[pl.BlockSpec(memory_space=pltpu.VMEM)] * count,
+        out_specs=[pl.BlockSpec(memory_space=pl.ANY)] * count,
+        scratch_shapes=[ring, ring, cores, cores, pltpu.SemaphoreType.DMA((count,))],
+        compiler_params=pltpu.CompilerParams(collective_id=ident, has_side_effects=True),
+        name=f"gather_{ident}",
+    )(*arrays)
+
+
+def reduce_kernel(count, chips, *refs):
+    part, out = refs[:count], refs[count : 2 * count]
+    pre, stage, got = refs[2 * count : 5 * count : 3], refs[2 * count + 1 : 5 * count : 3], refs[2 * count + 2 : 5 * count : 3]
+    core_send, core_recv, chip_send, chip_recv = refs[5 * count :]
+    me = lax.axis_index("tp")
+    chip, core = me // 2, me % 2
+    partner = chip * 2 + 1 - core
+    away = [(chip + o) % chips for o in range(1, chips)]
+    greet([partner] + [other * 2 + core for other in away])
+
+    def swap(k):
+        return remote(part[k].at[1 - core], pre[k], core_send.at[k], core_recv.at[k], partner)
+
+    def ship(k, o):
+        return remote(
+            stage[k].at[away[o]], got[k].at[o], chip_send.at[k, o], chip_recv.at[k, o], away[o] * 2 + core
+        )
+
+    for k in range(count):
+        swap(k).start()
+    for k in range(count):
+        swap(k).wait()
+
+        def add(q, _):
+            stage[k][q] = (
+                part[k][core, q].astype(jnp.float32) + pre[k][q].astype(jnp.float32)
+            ).astype(BF)
+            return 0
+
+        lax.fori_loop(0, chips, add, 0)
+        for o in range(chips - 1):
+            ship(k, o).start()
+    for k in range(count):
+        for o in range(chips - 1):
+            ship(k, o).wait()
+        total = stage[k][chip].astype(jnp.float32)
+        for o in range(chips - 1):
+            total = total + got[k][o].astype(jnp.float32)
+        out[k][...] = total.astype(BF)
+
+
+def reduce_pieces(partials, ident):
+    size = lax.axis_size("tp")
+    chips, count = size // 2, len(partials)
+    rows, width = partials[0].shape[0], partials[0].shape[1] // size
+    cut = [p.reshape(rows, chips, 2, width).transpose(2, 1, 0, 3) for p in partials]
+    held = pltpu.VMEM((chips, rows, width), BF)
+    got = pltpu.VMEM((chips - 1, rows, width), BF)
+    return pl.pallas_call(
+        functools.partial(reduce_kernel, count, chips),
+        out_shape=[jax.ShapeDtypeStruct((rows, width), BF)] * count,
+        in_specs=[pl.BlockSpec(memory_space=pltpu.VMEM)] * count,
+        out_specs=[pl.BlockSpec(memory_space=pltpu.VMEM)] * count,
+        scratch_shapes=[held, held, got] * count
+        + [pltpu.SemaphoreType.DMA((count,))] * 2
+        + [pltpu.SemaphoreType.DMA((count, chips - 1))] * 2,
+        compiler_params=pltpu.CompilerParams(
+            collective_id=ident, has_side_effects=True, vmem_limit_bytes=48 << 20
+        ),
+        name=f"reduce_{ident}",
+    )(*cut)
+
+
+def rows_kernel(x_ref, g_ref, o_ref):
+    o_ref[...] = jnp.dot(x_ref[...], g_ref[0], preferred_element_type=jnp.float32).astype(BF)
+
+
+def row_grads(x_turned, blocks):
+    features, rows = x_turned.shape
+    size, _, hidden = blocks.shape
+    return pl.pallas_call(
+        rows_kernel,
+        grid=(size,),
+        out_shape=jax.ShapeDtypeStruct((features, size * hidden), BF),
+        in_specs=[
+            pl.BlockSpec((features, rows), lambda n: (0, 0)),
+            pl.BlockSpec((1, rows, hidden), lambda n: (n, 0, 0)),
+        ],
+        out_specs=pl.BlockSpec((features, hidden), lambda n: (0, n)),
+        name="row_grads",
+        cost_estimate=pl.CostEstimate(
+            flops=2 * features * rows * size * hidden,
+            bytes_accessed=2 * size * hidden * (rows + features),
+            transcendentals=0,
+        ),
+    )(x_turned, blocks)
+
+
+def side_by_side(blocks):
+    size, rows, width = blocks.shape
+    return blocks.transpose(1, 0, 2).reshape(rows, size * width)
 
 
 def silu_parts(gate_pre):
@@ -64,16 +303,27 @@
         ),
     )
     recv_rows = recv_rows.reshape(buffer_rows, piece_width)
-    piece = lax.all_gather(recv_rows, "tp", axis=1, tiled=True)
+    recv_grad = recv_grad.reshape(buffer_rows, piece_width)
+    x_blocks, dy_blocks = gather([recv_rows, recv_grad], 0)
+    piece, dy_full = side_by_side(x_blocks), side_by_side(dy_blocks)
     gate_pre = jnp.dot(piece, gate_weight, preferred_element_type=jnp.float32)
     up_pre = jnp.dot(piece, up_weight, preferred_element_type=jnp.float32)
-    recv_grad = recv_grad.reshape(buffer_rows, piece_width)
     active, slope = silu_parts(gate_pre)
     hidden = (active * up_pre).astype(jnp.bfloat16)
     partial_value = jnp.dot(hidden, down_weight, preferred_element_type=jnp.float32)
-    out_piece = lax.psum_scatter(
-        partial_value.astype(jnp.bfloat16), "tp", scatter_dimension=1, tiled=True
-    )
+    grad_hidden = contract_cols(dy_full, down_weight)
+    grad_gate_pre = (grad_hidden * up_pre * slope).astype(jnp.bfloat16)
+    grad_up_pre = (grad_hidden * active).astype(jnp.bfloat16)
+    input_partial = contract_cols(grad_gate_pre, gate_weight) + contract_cols(
+        grad_up_pre, up_weight
+    )
+    out_piece, input_piece = reduce_pieces(
+        [partial_value.astype(jnp.bfloat16), input_partial.astype(jnp.bfloat16)], 1
+    )
+    hidden_in, gate_in, up_in, out_piece, input_piece = lax.optimization_barrier(
+        (hidden, grad_gate_pre, grad_up_pre, out_piece, input_piece)
+    )
+    hidden_blocks, gate_blocks, up_blocks = gather([hidden_in, gate_in, up_in], 2)
     out_back = lax.all_to_all(
         out_piece.reshape(groups, capacity, piece_width),
         "ep",
@@ -89,15 +339,6 @@
     mixed = jnp.sum(combine_weights[:, :, None] * out_tokens, axis=1).astype(jnp.bfloat16)
     local_products = jnp.sum(cotangent.astype(jnp.float32)[:, None, :] * out_tokens, axis=2)
     grad_combine = lax.psum(local_products, "tp")
-    grad_hidden = contract_cols(lax.all_gather(recv_grad, "tp", axis=1, tiled=True), down_weight)
-    grad_gate_pre = (grad_hidden * up_pre * slope).astype(jnp.bfloat16)
-    grad_up_pre = (grad_hidden * active).astype(jnp.bfloat16)
-    input_partial = contract_cols(grad_gate_pre, gate_weight) + contract_cols(
-        grad_up_pre, up_weight
-    )
-    input_piece = lax.psum_scatter(
-        input_partial.astype(jnp.bfloat16), "tp", scatter_dimension=1, tiled=True
-    )
     input_back = lax.all_to_all(
         input_piece.reshape(groups, capacity, piece_width),
         "ep",
@@ -111,15 +352,14 @@
         .astype(jnp.float32),
         axis=1,
     ).astype(jnp.bfloat16)
-    down_cols_out = contract_rows(
-        lax.all_gather(hidden, "tp", axis=1, tiled=True), recv_grad
-    ).astype(jnp.bfloat16)
-    gate_rows_out = contract_rows(
-        recv_rows, lax.all_gather(grad_gate_pre, "tp", axis=1, tiled=True)
-    ).astype(jnp.bfloat16)
-    up_rows_out = contract_rows(
-        recv_rows, lax.all_gather(grad_up_pre, "tp", axis=1, tiled=True)
-    ).astype(jnp.bfloat16)
+    down_cols_out = (
+        jnp.einsum("nrh,rd->nhd", hidden_blocks, recv_grad, preferred_element_type=jnp.float32)
+        .astype(jnp.bfloat16)
+        .reshape(-1, piece_width)
+    )
+    x_turned = recv_rows.T
+    gate_rows_out = row_grads(x_turned, gate_blocks)
+    up_rows_out = row_grads(x_turned, up_blocks)
     return (
         mixed,
         grad_tokens,

time: 346 us -> 261 us (0.75)
  waiting for transfers between devices: 189 us -> 11.4 us
  Pallas kernels: 0 us -> 139 us
  matrix products: 63.6 us -> 37.1 us
  blocking collectives: 49.5 us -> 24.3 us
  between operations: 14.3 us -> 0.99 us
  local copies, waits for them, and re-layouts: 15 us -> 24.5 us
  starting transfers between devices: 9.68 us -> 18.1 us
    pallas_call x0 -> x5, Pallas kernels: none -> 139 us  [the longest x2 91.6 us: gather(): pl.pallas_call(functools.partial(gather_kernel, count, chips), out_shape=...]
    all_gather x5 -> x0, waiting for transfers between devices: 107 us -> none  [the longest x1 34 us: body(): lax.all_gather(hidden, 'tp', axis=1, tiled=True)]
    unnamed x9 -> x0, waiting for transfers between devices: 74.4 us -> none
    all_to_all x2 -> x0, blocking collectives: 25.6 us -> none  [the longest x1 14.8 us: body(): lax.all_to_all(send_grad.reshape(groups, capacity, piece_width), 'ep', sp...]
    dot_general x3 -> x1, matrix products: 26.6 us -> 9.24 us  [body(): jnp.einsum('nrh,rd->nhd', hidden_blocks, recv_grad, preferred_element_typ...]
    reshape x0 -> x5, local copies, waits for them, and re-layouts: none -> 14 us  [the longest x2 10.7 us: reduce_pieces(): p.reshape(rows, chips, 2, width).transpose(2, 1, 0, 3)]
    all_to_all x0 -> x2, waiting for transfers between devices: none -> 11.4 us  [the longest x1 5.98 us: body(): lax.all_to_all(send_grad.reshape(groups, capacity, piece_width), 'ep', sp...]
    all_to_all x0 -> x2, starting transfers between devices: none -> 9.74 us  [the longest x1 6.35 us: body(): lax.all_to_all(send_rows.reshape(groups, capacity, piece_width), 'ep', sp...]
  transfers between devices with their start and end apart: 9 -> 4, of which waited for: 8 -> 2; matrix products, arithmetic and copies ran while one was open for 12% -> 6% of each run, Pallas kernels for 0% -> 34%
where the time goes in v2:
time: 261 us; the launch traced here: 260 us
  Pallas kernels  139 us (53%)
  matrix products  37.1 us (14%)
  local copies, waits for them, and re-layouts  24.5 us (9%)
  blocking collectives  24.3 us (9%)
  starting transfers between devices  18.1 us (7%)
  waiting for transfers between devices  11.4 us (4%)
  other arithmetic  4.56 us (2%)
    pallas_call x2, Pallas kernels, gather(): pl.pallas_call(functools.partial(gather_kernel, count, chips), out_shape=...  91.6 us
    pallas_call x1, Pallas kernels, reduce_pieces(): pl.pallas_call(functools.partial(reduce_kernel, count, chips), out_shape=...  28.8 us
    psum x1, blocking collectives, body(): grad_combine = lax.psum(local_products, 'tp')  24.3 us
    pallas_call x2, Pallas kernels, row_grads(): pl.pallas_call(rows_kernel, grid=(size,), out_shape=jax.ShapeDtypeStruct(...  18.3 us
    dot_general x3, matrix products, contract_cols(): lax.dot_general(left, right, (((1,), (1,)), ((), ())), preferred_element_...  15 us
    reshape x2, local copies, waits for them, and re-layouts, reduce_pieces(): p.reshape(rows, chips, 2, width).transpose(2, 1, 0, 3)  10.7 us
    dot_general x1, matrix products, body(): jnp.einsum('nrh,rd->nhd', hidden_blocks, recv_grad, preferred_element_typ...  9.24 us
    all_to_all x1, starting transfers between devices, body(): lax.all_to_all(send_rows.reshape(groups, capacity, piece_width), 'ep', sp...  6.35 us
  transfers between devices with their start and end apart: 4, of which 2 were waited for; matrix products, arithmetic and copies ran while one was open for 6% of the time, Pallas kernels for 34%

profile of v2, /device:TPU:0, one launch (start us, length us, event | category | flops | bytes accessed | tf_op | source)
XLA Modules:
  0.0 259.6 jit_solution(8967369403870925718)
XLA Ops:
  1.6 1.2 reduce-window.6
  4.3 1.0 convolution_convert_fusion.2
  5.3 6.3 %all-to-all-start = ((bf16[4,80,384]{2,1,0:T(8,128)(2,1)}), bf16[4,80,384]{2,1,0:T(8,128)(2,1)S(1)}, u32[]{:S(2)}, u32[]{:S(2)}) async-start(bf16[4,80,384]{2,1,0:T(8,128)(2,1)} %bitcast.2), calls=%async_computation | async-start | bytes 491520 | tf_op jit(solution)/shard_map/all_to_all | solution.py:290
  12.5 1.0 mul.80
  13.7 1.0 convolution_convert_fusion.1
  14.7 5.4 %all-to-all-done = bf16[4,80,384]{2,1,0:T(8,128)(2,1)S(1)} async-done(((bf16[4,80,384]{2,1,0:T(8,128)(2,1)}), bf16[4,80,384]{2,1,0:T(8,128)(2,1)S(1)}, u32[]{:S(2)}, u32[]{:S(2)}) %all-to-all-start) | async-done | bytes 245792 | tf_op jit(solution)/shard_map/all_to_all | solution.py:290
  20.2 3.4 %all-to-all-start.1 = ((bf16[4,80,384]{2,1,0:T(8,128)(2,1)}), bf16[4,80,384]{2,1,0:T(8,128)(2,1)S(1)}, u32[]{:S(2)}, u32[]{:S(2)}) async-start(bf16[4,80,384]{2,1,0:T(8,128)(2,1)} %bitcast.4), calls=%async_computation.1 | async-start | bytes 491520 | tf_op jit(solution)/shard_map/all_to_all | solution.py:297
  23.6 0.9 copy.56
  24.5 6.0 %all-to-all-done.1 = bf16[4,80,384]{2,1,0:T(8,128)(2,1)S(1)} async-done(((bf16[4,80,384]{2,1,0:T(8,128)(2,1)}), bf16[4,80,384]{2,1,0:T(8,128)(2,1)S(1)}, u32[]{:S(2)}, u32[]{:S(2)}) %all-to-all-start.1) | async-done | bytes 245792 | tf_op jit(solution)/shard_map/all_to_all | solution.py:297
  31.2 21.8 %gather_0.1 = (bf16[8,320,384]{2,1,0:T(8,128)(2,1)}, bf16[8,320,384]{2,1,0:T(8,128)(2,1)}) custom-call(bf16[320,384]{1,0:T(8,128)(2,1)} %bitcast.73, bf16[320,384]{1,0:T(8,128)(2,1)} %bitcast.79), custom_call_target="tpu_custom_call" | custom-call | tf_op jit(solution)/shard_map/gather_0/pallas_call | solution.py:142
  53.0 2.0 copy.58
  55.5 5.2 %fusion.6 = f32[320,1024]{1,0:T(8,128)S(1)} fusion(bf16[320,3072]{1,0:T(8,128)(2,1)S(1)} %bitcast.75, bf16[1,3072,1024]{2,1,0:T(8,128)(2,1)} %param.14), kind=kOutput, calls=%fused_computation.8 | convolution fusion | flops 2013265920 | bytes 9568256 | tf_op jit(solution)/shard_map/dot_general | solution.py:310
  60.7 2.2 fusion.10
  63.0 3.6 %multiply_convert_fusion = (bf16[320,1024]{1,0:T(8,128)(2,1)S(1)}, bf16[320,1024]{1,0:T(8,128)(2,1)}, bf16[320,1024]{1,0:T(8,128)(2,1)S(1)}) fusion(f32[320,1024]{1,0:T(8,128)S(1)} %fusion.10, f32[320,1024]{1,0:T(8,128)S(1)} %fusion.6, bf16[320,3072]{1,0:T(8,128)(2,1)S(1)} %bitcast.74, bf16[1,1024,3072]{2,1,0:T(8,128)(2,1)S(1)} %bitcast.84), kind=kOutput, calls=%fused_computation.20 | convolution fusion | flops 2018181120 | bytes 12845056 | tf_op jit(solution)/shard_map/dot_general | solution.py:258
  67.4 3.5 %fusion.18 = bf16[320,3072]{1,0:T(8,128)(2,1)} fusion(bf16[320,1024]{1,0:T(8,128)(2,1)S(1)} %get-tuple-element.25.refs_0_, bf16[1,1024,3072]{2,1,0:T(8,128)(2,1)S(1)} %bitcast.84), kind=kOutput, calls=%fused_computation.16 | convolution fusion | flops 2014248960 | bytes 8912896 | tf_op jit(solution)/shard_map/dot_general | solution.py:313
  70.9 5.0 %reshape.107 = bf16[320,4,2,384]{3,2,1,0:T(2,128)(2,1)S(1)} reshape(bf16[320,3072]{1,0:T(8,128)(2,1)} %fusion.18) | data formatting | bytes 3932160 | tf_op jit(solution)/shard_map/reshape | solution.py:198
  75.9 5.1 %fusion.4 = f32[320,3072]{1,0:T(8,128)S(1)} fusion(bf16[320,1024]{1,0:T(8,128)(2,1)S(1)} %get-tuple-element.27.refs_2_, bf16[1,3072,1024]{2,1,0:T(8,128)(2,1)} %param.14), kind=kOutput, calls=%fused_computation.6 | convolution fusion | flops 2013265920 | bytes 10878976 | tf_op jit(solution)/shard_map/dot_general | solution.py:258
  81.0 6.4 %fusion.15 = bf16[320,3072]{1,0:T(8,128)(2,1)} fusion(f32[320,3072]{1,0:T(8,128)S(1)} %fusion.4, bf16[320,1024]{1,0:T(8,128)(2,1)S(1)} %copy-done.7, bf16[1,3072,1024]{2,1,0:T(8,128)(2,1)} %param.13), kind=kOutput, calls=%fused_computation.15 | convolution fusion | flops 2015232000 | bytes 12845056 | tf_op jit(solution)/shard_map/dot_general | solution.py:258
  87.4 5.7 %reshape.108 = bf16[320,4,2,384]{3,2,1,0:T(2,128)(2,1)} reshape(bf16[320,3072]{1,0:T(8,128)(2,1)} %fusion.15) | data formatting | bytes 3932160 | tf_op jit(solution)/shard_map/reshape | solution.py:198
  93.1 2.2 copy_bitcast_fusion
  95.3 28.8 %reduce_1.1 = (bf16[320,384]{1,0:T(8,128)(2,1)}, bf16[320,384]{1,0:T(8,128)(2,1)}) custom-call(bf16[2,4,320,384]{3,2,1,0:T(8,128)(2,1)S(1)} %get-tuple-element.57.refs_0_, bf16[2,4,320,384]{3,2,1,0:T(8,128)(2,1)S(1)} %get-tuple-element.56.refs_1_), custom_call_target="tpu_custom_call" | custom-call | tf_op jit(solution)/shard_map/reduce_1/pallas_call | solution.py:201
  124.1 3.5 %all-to-all-start.3 = ((bf16[4,80,384]{2,1,0:T(8,128)(2,1)}), bf16[4,80,384]{2,1,0:T(8,128)(2,1)S(1)}, u32[]{:S(2)}, u32[]{:S(2)}) async-start(bf16[4,80,384]{2,1,0:T(8,128)(2,1)} %bitcast.15), calls=%async_computation.3 | async-start | bytes 491520 | tf_op jit(solution)/shard_map/all_to_all | solution.py:342
  127.7 69.8 %gather_2.1 = (bf16[8,320,1024]{2,1,0:T(8,128)(2,1)}, bf16[8,320,1024]{2,1,0:T(8,128)(2,1)}, bf16[8,320,1024]{2,1,0:T(8,128)(2,1)}) custom-call(bf16[320,1024]{1,0:T(8,128)(2,1)} %copy-done.8, bf16[320,1024]{1,0:T(8,128)(2,1)} %get-tuple-element.26.refs_1_, bf16[320,1024]{1,0:T(8,128)(2,1)} %copy-done.6), custom_call_target="tpu_custom_call" | custom-call | tf_op jit(solution)/shard_map/gather_2/pallas_call | solution.py:142
  197.5 9.2 %convolution_convert_fusion = bf16[8,1024,384]{2,1,0:T(8,128)(2,1)} fusion(bf16[8,320,1024]{2,1,0:T(8,128)(2,1)} %get-tuple-element.30, bf16[320,384,1]{1,0,2:T(8,128)(2,1)S(1)} %bitcast.80), kind=kOutput, calls=%fused_computation.17 | convolution fusion | flops 2016411648 | bytes 11780096 | tf_op jit(solution)/shard_map/nrh,rd->nhd/dot_general | solution.py:356
  206.7 4.8 %all-to-all-start.2 = ((bf16[4,80,384]{2,1,0:T(8,128)(2,1)}), bf16[4,80,384]{2,1,0:T(8,128)(2,1)S(1)}, u32[]{:S(2)}, u32[]{:S(2)}) async-start(bf16[4,80,384]{2,1,0:T(8,128)(2,1)} %bitcast.13), calls=%async_computation.2 | async-start | bytes 491520 | tf_op jit(solution)/shard_map/all_to_all | solution.py:327
  211.6 9.2 %row_grads.2 = bf16[384,8192]{1,0:T(8,128)(2,1)} custom-call(bf16[384,320]{1,0:T(8,128)(2,1)} %bitcast.70, bf16[8,320,1024]{2,1,0:T(8,128)(2,1)} %get-tuple-element.28.g_ref), custom_call_target="tpu_custom_call" | custom-call | flops 2013265920 | bytes 11534336 | tf_op jit(solution)/shard_map/row_grads/pallas_call | solution.py:223
  220.7 9.2 %row_grads.3 = bf16[384,8192]{1,0:T(8,128)(2,1)} custom-call(bf16[384,320]{1,0:T(8,128)(2,1)} %bitcast.71, bf16[8,320,1024]{2,1,0:T(8,128)(2,1)} %get-tuple-element.29.g_ref), custom_call_target="tpu_custom_call" | custom-call | flops 2013265920 | bytes 11534336 | tf_op jit(solution)/shard_map/row_grads/pallas_call | solution.py:223
  229.9 1.0 gather_fusion.1
  230.9 1.0 gather_fusion
  232.3 24.3 %psum.7 = f32[96,2]{1,0:T(8,128)S(1)} all-reduce(f32[96,2]{1,0:T(8,128)S(1)} %reduce_sum.61), channel_id=1, replica_groups=mesh['ep'=4,'tp'=8] {'tp'}, use_global_device_ids=true, to_apply=%region_7.9 | all-reduce | flops 192 | bytes 1536 | tf_op jit(solution)/shard_map/psum | solution.py:341
  257.5 1.1 multiply_reduce_fusion.1
  258.6 1.0 reduce_sum.59
  (60 shorter events, 6.9 us)
Async XLA Ops:
  0.6 3.7 %copy-start = (bf16[96,384]{1,0:T(8,128)(2,1)S(1)}, bf16[96,384]{1,0:T(8,128)(2,1)}, u32[]{:S(2)}) copy-start(bf16[96,384]{1,0:T(8,128)(2,1)} %param.9) | copy-start | bytes 221188
  5.3 14.9 %all-to-all-start = ((bf16[4,80,384]{2,1,0:T(8,128)(2,1)}), bf16[4,80,384]{2,1,0:T(8,128)(2,1)S(1)}, u32[]{:S(2)}, u32[]{:S(2)}) async-start(bf16[4,80,384]{2,1,0:T(8,128)(2,1)} %bitcast.2), calls=%async_computation | async-start | bytes 491520 | tf_op jit(solution)/shard_map/all_to_all | solution.py:290
  20.2 10.3 %copy-start.2 = (bf16[4,80,384]{2,1,0:T(8,128)(2,1)}, bf16[4,80,384]{2,1,0:T(8,128)(2,1)S(1)}, u32[]{:S(2)}) copy-start(bf16[4,80,384]{2,1,0:T(8,128)(2,1)S(1)} %all-to-all-done) | copy-start | bytes 737284
  20.2 10.3 %all-to-all-start.1 = ((bf16[4,80,384]{2,1,0:T(8,128)(2,1)}), bf16[4,80,384]{2,1,0:T(8,128)(2,1)S(1)}, u32[]{:S(2)}, u32[]{:S(2)}) async-start(bf16[4,80,384]{2,1,0:T(8,128)(2,1)} %bitcast.4), calls=%async_computation.1 | async-start | bytes 491520 | tf_op jit(solution)/shard_map/all_to_all | solution.py:297
  30.5 0.7 copy-start.4
  53.0 2.1 copy-start.3
  55.1 5.6 %slice-start.2 = ((s8[6291456]{0:T(1024)(128)(4,1)}), s8[2097152]{0:T(1024)(128)(4,1)S(1)}, s32[]{:S(2)}) async-start(s8[6291456]{0:T(1024)(128)(4,1)} %bitcast.85), calls=%async_computation.6 | async-start | bytes 4194304
  55.5 5.2 %slice-start.3 = ((s8[6291456]{0:T(1024)(128)(4,1)}), s8[4194304]{0:T(1024)(128)(4,1)S(1)}, s32[]{:S(2)}) async-start(s8[6291456]{0:T(1024)(128)(4,1)} %bitcast.85), calls=%async_computation.7 | async-start | bytes 8388608
  55.5 7.4 %slice-start = ((s8[6291456]{0:T(1024)(128)(4,1)}), s8[4194304]{0:T(1024)(128)(4,1)S(1)}, s32[]{:S(2)}) async-start(s8[6291456]{0:T(1024)(128)(4,1)} %bitcast.83), calls=%async_computation.4 | async-start | bytes 8388608
  60.7 2.2 slice-start.1
  66.5 0.9 copy-start.8
  66.5 9.4 %copy-start.6 = (bf16[320,1024]{1,0:T(8,128)(2,1)}, bf16[320,1024]{1,0:T(8,128)(2,1)S(1)}, u32[]{:S(2)}) copy-start(bf16[320,1024]{1,0:T(8,128)(2,1)S(1)} %get-tuple-element.27.refs_2_) | copy-start | bytes 1966084
  75.9 5.1 %copy-start.7 = (bf16[320,1024]{1,0:T(8,128)(2,1)S(1)}, bf16[320,1024]{1,0:T(8,128)(2,1)}, u32[]{:S(2)}) copy-start(bf16[320,1024]{1,0:T(8,128)(2,1)} %get-tuple-element.26.refs_1_) | copy-start | bytes 1966084
  124.1 73.4 %copy-start.5 = (bf16[4,80,384]{2,1,0:T(8,128)(2,1)S(1)}, bf16[4,80,384]{2,1,0:T(8,128)(2,1)}, u32[]{:S(2)}) copy-start(bf16[4,80,384]{2,1,0:T(8,128)(2,1)} %copy-done.4) | copy-start | bytes 737284
  124.1 82.6 %all-to-all-start.3 = ((bf16[4,80,384]{2,1,0:T(8,128)(2,1)}), bf16[4,80,384]{2,1,0:T(8,128)(2,1)S(1)}, u32[]{:S(2)}, u32[]{:S(2)}) async-start(bf16[4,80,384]{2,1,0:T(8,128)(2,1)} %bitcast.15), calls=%async_computation.3 | async-start | bytes 491520 | tf_op jit(solution)/shard_map/all_to_all | solution.py:342
  206.7 24.2 %all-to-all-start.2 = ((bf16[4,80,384]{2,1,0:T(8,128)(2,1)}), bf16[4,80,384]{2,1,0:T(8,128)(2,1)S(1)}, u32[]{:S(2)}, u32[]{:S(2)}) async-start(bf16[4,80,384]{2,1,0:T(8,128)(2,1)} %bitcast.13), calls=%async_computation.2 | async-start | bytes 491520 | tf_op jit(solution)/shard_map/all_to_all | solution.py:327
  230.9 28.7 %copy-start.1 = (bf16[96,384]{1,0:T(8,128)(2,1)S(1)}, bf16[96,384]{1,0:T(8,128)(2,1)}, u32[]{:S(2)}) copy-start(bf16[96,384]{1,0:T(8,128)(2,1)} %param.9) | copy-start | bytes 221188
